TPU v7x, 32 devices: a whole 2x2x4 slice. The times are simulated.
32 devices in a mesh: expert: 8 (over z, y), vocab: 4 (over x, core).
Axes of the slice: x: 2, y: 2, z: 4, core: 2. Of those that a mesh axis runs over, the one named last changes fastest.
Arguments:
- tokens: bfloat16 [1024, 2048], P('expert'), may hold values from -12 to 12
- expert_ids: int32 [1024, 6], P('expert'), may hold values from 0 to 15, all different within a row; in each aligned block of 128 rows (0 to 127, 128 to 255, ...) at most 96 rows name the same one
- gates: float32 [1024, 6], P('expert'), may hold values from 0.05 to 0.4
- w_gate: bfloat16 [16, 2048, 1408], P('expert', None, 'vocab'), may hold values from -0.125 to 0.125
- w_up: bfloat16 [16, 2048, 1408], P('expert', None, 'vocab'), may hold values from -0.125 to 0.125
- w_down: bfloat16 [16, 1408, 2048], P('expert', 'vocab'), may hold values from -0.21875 to 0.21875
- norm_gain: float32 [2048], replicated, may hold values from 0.5 to 1.5
- lm_weight: bfloat16 [2048, 24576], P(None, ('expert', 'vocab')), may hold values from -6.9605824 to 6.9605824
- targets: int32 [1024], P('expert'), may hold values from 0 to 24575
Outputs:
- logprobs: float32 [1024], P('expert')
Inputs may be any that keep to these rules, and one draw needn't show every extreme that they name: `expert_ids`: in the 128 rows of one device no expert is named by more than 96 routes; each row names 6 different experts.
All inputs are finite; a program needn't handle non-finite values.
Results may differ from a plain program's by a relative error of at most 0.003.
Values may be sent and summed in bfloat16 or wider, within the bound.
No kernel may reach another device: no remote copies, remote signals or barrier semaphores. Data moves between devices by JAX's collectives and lax.ppermute only.
A program may use at most 128 MiB of HBM per device.

v0:
```python
import functools

import jax
import jax.numpy as jnp
from jax import lax
from jax.experimental import pallas as pl
from jax.experimental.pallas import tpu as pltpu
from jax.sharding import PartitionSpec as P


AXES = ("expert", "vocab")
LANES = 128


def chip_bytes(mebibytes, rows):
    return min(56, mebibytes * max(1, rows // 256)) * 2**20


def exchange(value, masks):
    devices = lax.axis_size(AXES)
    return lax.ppermute(value, AXES, [(d, d ^ masks[d & 1]) for d in range(devices)])


def gather_far(own, bits):
    parts = own
    rows = own.shape[0]
    for bit in bits:
        pieces = [parts[:rows], parts[rows:]] if parts.shape[0] > rows else [parts]
        parts = jnp.concatenate([parts] + [exchange(p, (1 << bit,) * 2) for p in pieces], axis=0)
    return parts


def reduce_far(total, bits, rows):
    for bit in reversed(bits):
        keep = total.shape[0] // 2
        far = total[keep:].astype(jnp.bfloat16)
        cuts = (keep // 2, 0) if keep > rows else (0,)
        ends = (keep, keep // 2) if keep > rows else (keep,)
        got = [exchange(far[lo:hi], (1 << bit,) * 2).astype(jnp.float32) for lo, hi in zip(cuts, ends)]
        near = [total[lo:hi] + g for lo, hi, g in zip(cuts, ends, got)]
        total = jnp.concatenate(near[::-1], axis=0) if len(near) > 1 else near[0]
    return total


def pack_kernel(place_ref, tokens_hbm, ids_hbm, gates_hbm, targets_hbm, out_ref,
                tokens_ref, ids_ref, gates_ref, targets_ref, sems):
    own, total = out_ref.shape
    width = tokens_ref.shape[1]
    first = pl.multiple_of(place_ref[0] * own, own)
    experts_all = place_ref[2]
    copies = [
        pltpu.make_async_copy(src, dst, sems.at[i])
        for i, (src, dst) in enumerate((
            (tokens_hbm.at[pl.ds(first, own)], tokens_ref),
            (ids_hbm, ids_ref),
            (gates_hbm, gates_ref),
            (targets_hbm, targets_ref),
        ))
    ]
    for copy in copies:
        copy.start()
    for copy in copies:
        copy.wait()
    out_ref[:, :width] = tokens_ref[...]
    shape = (own, total - width)
    lane = lax.broadcasted_iota(jnp.int32, shape, 1)
    row = lax.broadcasted_iota(jnp.int32, (own, targets_ref.shape[1]), 0)
    column = lax.broadcasted_iota(jnp.int32, (own, targets_ref.shape[1]), 1)

    def turned(values):
        return jnp.sum(jnp.where(column == row + first, values, 0.0), axis=1, keepdims=True)

    low = lane >= experts_all
    expert = jnp.where(low, lane - experts_all, lane).astype(jnp.float32)
    coef = jnp.zeros(shape, jnp.float32)
    for k in range(ids_ref.shape[0]):
        chosen = turned(ids_ref[k : k + 1].astype(jnp.float32))
        coef = jnp.where(expert == chosen, turned(gates_ref[k : k + 1]), coef)
    high = coef.astype(jnp.bfloat16).astype(jnp.float32)
    value = jnp.where(low, coef - high, high)
    token = targets_ref[...]
    digits = (token // 16384, (token // 128) % 128, token % 128)
    for j, digit in enumerate(digits):
        value = jnp.where(lane == 2 * experts_all + j, turned(digit.astype(jnp.float32)), value)
    value = jnp.where(lane < 2 * experts_all + len(digits), value, 0.0)
    out_ref[:, width:] = value.astype(jnp.bfloat16)


def packed(place, tokens, expert_ids, gates, targets, own, extra):
    vmem = pl.BlockSpec(memory_space=pltpu.VMEM)
    return pl.pallas_call(
        pack_kernel,
        out_shape=jax.ShapeDtypeStruct((own, tokens.shape[1] + extra), jnp.bfloat16),
        in_specs=[pl.BlockSpec(memory_space=pltpu.SMEM)] + [pl.BlockSpec(memory_space=pl.ANY)] * 4,
        out_specs=vmem,
        scratch_shapes=[
            pltpu.VMEM((own, tokens.shape[1]), tokens.dtype),
            pltpu.VMEM(expert_ids.shape, expert_ids.dtype),
            pltpu.VMEM(gates.shape, gates.dtype),
            pltpu.VMEM(targets.shape, targets.dtype),
            pltpu.SemaphoreType.DMA((4,)),
        ],
        compiler_params=pltpu.CompilerParams(vmem_limit_bytes=4 * 2**20),
        name="pack",
    )(place, tokens, expert_ids, gates, targets)


def touch_kernel(place_ref, *refs):
    for i in range(place_ref.shape[0]):
        refs[-1][i] = place_ref[i]


def touched(place, matrices):
    vmem = pl.BlockSpec(memory_space=pltpu.VMEM)
    smem = pl.BlockSpec(memory_space=pltpu.SMEM)
    return pl.pallas_call(
        touch_kernel,
        out_shape=jax.ShapeDtypeStruct(place.shape, place.dtype),
        in_specs=[smem] + [vmem] * len(matrices),
        out_specs=smem,
        compiler_params=pltpu.CompilerParams(vmem_limit_bytes=2**20),
        name="touch",
    )(place, *matrices)


def expert_kernel(place_ref, *refs, groups):
    pieces = refs[:-8]
    gate_ref, up_ref, down_ref, near_out, away_out, info_out, x_ref, hidden_ref = refs[-8:]
    units, width = down_ref.shape
    hid = units // groups
    rows = near_out.shape[0]
    piece = pieces[0].shape[0]
    for i, ref in enumerate(pieces):
        x_ref[i * piece : (i + 1) * piece] = ref[:, :width]
        info_out[i * piece : (i + 1) * piece] = ref[:, width:]
    table = info_out[...].astype(jnp.float32)
    lane = lax.broadcasted_iota(jnp.int32, table.shape, 1)
    every = place_ref[2]
    unit = lax.broadcasted_iota(jnp.int32, (1, units), 1)
    scale = jnp.zeros((2 * rows, units), jnp.float32)
    for l in range(groups):
        mine = place_ref[1] + l
        hit = (lane == mine) | (lane == mine + every)
        value = jnp.sum(jnp.where(hit, table, 0.0), axis=1, keepdims=True)
        scale = jnp.where((unit >= l * hid) & (unit < (l + 1) * hid), value, scale)
    dims = (((1,), (1,)), ((), ()))
    for lo in range(0, units, 256):
        part = slice(lo, min(lo + 256, units))
        gate_val = lax.dot_general(
            x_ref[...], gate_ref[part], dims, preferred_element_type=jnp.float32
        )
        up_val = lax.dot_general(x_ref[...], up_ref[part], dims, preferred_element_type=jnp.float32)
        hidden = gate_val / (1.0 + jnp.exp(-gate_val)) * up_val * scale[:, part]
        hidden_ref[:, part] = hidden.astype(jnp.bfloat16)
    result = jnp.dot(hidden_ref[...], down_ref[...], preferred_element_type=jnp.float32)
    near_out[...] = result[:rows]
    away_out[...] = result[rows:].astype(jnp.bfloat16)


def experts(place, pieces, matrices, groups):
    units, width = matrices[2].shape
    rows, total = len(pieces) // 2 * pieces[0].shape[0], pieces[0].shape[1]
    vmem = pl.BlockSpec(memory_space=pltpu.VMEM)
    return pl.pallas_call(
        functools.partial(expert_kernel, groups=groups),
        out_shape=(
            jax.ShapeDtypeStruct((rows, width), jnp.float32),
            jax.ShapeDtypeStruct((rows, width), jnp.bfloat16),
            jax.ShapeDtypeStruct((2 * rows, total - width), jnp.bfloat16),
        ),
        in_specs=[pl.BlockSpec(memory_space=pltpu.SMEM)] + [vmem] * (len(pieces) + 3),
        out_specs=(vmem, vmem, vmem),
        scratch_shapes=[
            pltpu.VMEM((2 * rows, width), jnp.bfloat16),
            pltpu.VMEM((2 * rows, units), jnp.bfloat16),
        ],
        cost_estimate=pl.CostEstimate(
            flops=12 * rows * units * width, transcendentals=2 * rows * units,
            bytes_accessed=6 * units * width,
        ),
        compiler_params=pltpu.CompilerParams(vmem_limit_bytes=chip_bytes(20, 2 * rows)),
        name="experts",
    )(place, *pieces, *matrices)


def stats_kernel(base_ref, *refs, digit):
    pieces = refs[:-3]
    info_ref, weight_ref, out_ref = refs[-3:]
    rows = out_ref.shape[1]
    weight = weight_ref[...]
    info = info_ref[...].astype(jnp.float32)
    lane = lax.broadcasted_iota(jnp.int32, info.shape, 1)
    place = jnp.zeros((rows, 1), jnp.float32)
    for j, worth in enumerate((16384.0, 128.0, 1.0)):
        place = place + worth * jnp.sum(
            jnp.where(lane == digit + j, info, 0.0), axis=1, keepdims=True
        )
    place = place.astype(jnp.int32) - base_ref[0]
    x = jnp.concatenate([ref[...] for ref in pieces], axis=0)
    logits = jnp.dot(x, weight, preferred_element_type=jnp.float32)
    column = lax.broadcasted_iota(jnp.int32, logits.shape, 1)
    top = jnp.max(logits, axis=1, keepdims=True)
    mass = jnp.sum(jnp.exp(logits - top), axis=1, keepdims=True)
    chosen = jnp.sum(jnp.where(column == place, logits, 0.0), axis=1, keepdims=True)
    wide = lax.broadcasted_iota(jnp.int32, (rows, LANES), 1)
    flat = jnp.where(wide == 0, top, jnp.where(wide == 1, mass, chosen))
    out_ref[...] = flat.T[:8]


def row_stats(base, pieces, info, weight, digit):
    rows = len(pieces) * pieces[0].shape[0]
    vmem = pl.BlockSpec(memory_space=pltpu.VMEM)
    return pl.pallas_call(
        functools.partial(stats_kernel, digit=digit),
        out_shape=jax.ShapeDtypeStruct((8, rows), jnp.float32),
        in_specs=[pl.BlockSpec(memory_space=pltpu.SMEM)] + [vmem] * (len(pieces) + 2),
        out_specs=vmem,
        cost_estimate=pl.CostEstimate(
            flops=2 * rows * weight.shape[0] * weight.shape[1],
            transcendentals=rows * weight.shape[1], bytes_accessed=2 * weight.size,
        ),
        compiler_params=pltpu.CompilerParams(vmem_limit_bytes=chip_bytes(12, rows)),
        name="stats",
    )(base, *pieces, info, weight)


def layer(tokens, expert_ids, gates, w_gate, w_up, w_down, norm_gain, lm_weight, targets):
    tok_rows, width = tokens.shape
    groups, _, hid = w_gate.shape
    expert_devs = lax.axis_size("expert")
    vocab_devs = lax.axis_size("vocab")
    devices = expert_devs * vocab_devs
    experts_all = groups * expert_devs
    bits = devices.bit_length() - 1
    vocab_bits = vocab_devs.bit_length() - 1
    own = tok_rows // vocab_devs
    vocab_index = lax.axis_index("vocab")
    expert_index = lax.axis_index("expert")

    used = 2 * experts_all + 3
    extra = -(-used // LANES) * LANES
    place = jnp.stack([vocab_index, expert_index * groups, experts_all]).astype(jnp.int32)
    payload = packed(place, tokens, expert_ids.T, gates.T, targets.reshape(1, -1), own, extra)
    tokens_own = payload[:, :width]

    far = list(range(bits - 1, vocab_bits, -1))
    step_a = (1 << vocab_bits, 2)
    step_b = (2, 1 << vocab_bits)
    near_swap = (1, 1)

    units = groups * hid
    matrices = (
        w_gate.swapaxes(1, 2).reshape(units, width),
        w_up.swapaxes(1, 2).reshape(units, width),
        w_down.reshape(units, width),
    )
    last = (1 << far[-1],) * 2

    def crossed(value):
        return exchange(value, near_swap)

    def spread(own_rows, work):
        early = gather_far(own_rows, far[:-1])[own:]
        middle = exchange(own_rows, last)
        final = exchange(early, last)
        done = []
        for g, start in enumerate((own_rows, jnp.concatenate([early, middle], 0), final)):
            one = exchange(start, step_a)
            two = exchange(start, step_b)
            both = exchange(one, step_b)
            calls = ((start, one), (two, both)) if g == 1 else ((start, one, two, both),)
            for near in calls:
                pieces = near + tuple(crossed(p) for p in near)
                done.append(work(pieces))
        return done

    def moved(value, masks):
        return exchange(value.astype(jnp.bfloat16), masks).astype(jnp.float32)

    def chip_part(pieces):
        return experts(place, pieces, matrices, groups)

    place = touched(touched(place, matrices[:2]), matrices[2:])
    parts = spread(payload, chip_part)
    totals = []
    for calls in (parts[:1], parts[1:3], parts[3:]):
        kept = [near + crossed(away).astype(jnp.float32) for near, away, _ in calls]
        size = kept[0].shape[0] * len(calls) // 4
        start, one, two, both = [k[i : i + size] for k in kept for i in range(0, len(k), size)]
        one = one + moved(both, step_b)
        start = start + moved(two, step_b)
        totals.append(start + moved(one, step_a))
    rest = totals[1][:-own] + moved(totals[2], last)
    total = totals[0] + moved(totals[1][-own:], last)
    if len(far) == 2:
        total = total + moved(rest, (1 << far[0],) * 2)
    else:
        total = reduce_far(jnp.concatenate([total, rest], 0), far[:-1], own)

    resid = (tokens_own.astype(jnp.float32) + total).astype(jnp.bfloat16)
    resid_f = resid.astype(jnp.float32)
    squares = jnp.mean(resid_f * resid_f, axis=1)
    normed = (resid_f * lax.rsqrt(squares + 1e-06)[:, None] * norm_gain[None, :]).astype(
        jnp.bfloat16
    )
    base = (expert_index * vocab_devs + vocab_index) * lm_weight.shape[1]
    base = base.reshape(1).astype(jnp.int32)

    def joined(first, second):
        best = jnp.maximum(first[0], second[0])
        mass = first[1] * jnp.exp(first[0] - best) + second[1] * jnp.exp(second[0] - best)
        return jnp.stack([best, mass, first[2] + second[2]])

    infos = iter([part[2] for part in parts])

    def chip_stats(pieces):
        return row_stats(base, pieces, next(infos), lm_weight, 2 * experts_all)

    got = [q[:3] for q in spread(normed, chip_stats)]
    table = jnp.concatenate(
        [
            got[0].reshape(3, 2, 2, 2, -1),
            jnp.stack([q.reshape(3, 2, 2, -1) for q in got[1:3]], axis=2),
            got[3].reshape(3, 2, 2, 2, -1),
        ],
        axis=4,
    )
    odd = vocab_index % 2
    table = jnp.stack(
        [
            jnp.where(odd == 0, table[:, 0], table[:, 0].swapaxes(1, 2)),
            jnp.where(odd == 1, table[:, 1], table[:, 1].swapaxes(1, 2)),
        ],
        axis=1,
    )
    table = joined(table, exchange(table[:, ::-1], near_swap))
    table = joined(table, exchange(table[:, :, ::-1], (2, 2)))
    table = table.reshape(3, 2, 2, 2, 1 << len(far), own).transpose(0, 3, 4, 1, 2, 5)
    table = table.reshape(3, 2 << len(far), 4, own)
    low = 1 << len(far)
    table = joined(table[:, :low], exchange(table[:, low:], (1 << vocab_bits,) * 2))
    for bit in reversed(far):
        low = low // 2
        table = joined(table[:, :low], exchange(table[:, low:], (1 << bit,) * 2))
    result = (table[2] - table[0] - jnp.log(table[1]))[0]
    share = jnp.arange(vocab_devs, dtype=jnp.int32)
    label = (share % 2) * 2 + share // 2
    ordered = jnp.sum(
        jnp.where(
            ((share[:, None] ^ vocab_index) == label[None, :])[:, :, None], result[None, :, :], 0.0
        ),
        axis=1,
    )
    return ordered.reshape(tok_rows)


def solution(mesh):
    in_specs = (
        P("expert", None),
        P("expert", None),
        P("expert", None),
        P("expert", None, "vocab"),
        P("expert", None, "vocab"),
        P("expert", "vocab", None),
        P(),
        P(None, ("expert", "vocab")),
        P("expert"),
    )
    return jax.shard_map(
        layer, mesh=mesh, in_specs=in_specs, out_specs=P("expert"), check_vma=False
    )
```

profile of v0, /device:TPU:0, one launch (start us, length us, event | category | flops | bytes accessed | tf_op | source)
XLA Modules:
  0.0 155.1 jit_solution(4847308751134382062)
XLA Ops:
  4.1 4.1 %collective-permute-start.11 = (bf16[32,2176]{1,0:T(8,128)(2,1)S(1)}, bf16[32,2176]{1,0:T(8,128)(2,1)S(1)}, u32[]{:S(2)}, u32[]{:S(2)}) collective-permute-start(bf16[32,2176]{1,0:T(8,128)(2,1)S(1)} %pack.1.refs_0_), channel_id=1, source_target_pairs={{0,16},{1,17},{2,18},{3,19},{4,20},{5,21},{6,22},{7,23},{8,24},{9,... | collective-permute-start | bytes 417800 | tf_op jit(solution)/shard_map/ppermute | solution.py:21
  12.8 2.2 %collective-permute-done.11 = bf16[32,2176]{1,0:T(8,128)(2,1)S(1)} collective-permute-done((bf16[32,2176]{1,0:T(8,128)(2,1)S(1)}, bf16[32,2176]{1,0:T(8,128)(2,1)S(1)}, u32[]{:S(2)}, u32[]{:S(2)}) %collective-permute-start.11) | collective-permute-done | bytes 139296 | tf_op jit(solution)/shard_map/ppermute | solution.py:21
  20.1 2.5 %collective-permute-done.2.refs_3_ = bf16[32,2176]{1,0:T(8,128)(2,1)S(1)} collective-permute-done((bf16[32,2176]{1,0:T(8,128)(2,1)S(1)}, bf16[32,2176]{1,0:T(8,128)(2,1)S(1)}, u32[]{:S(2)}, u32[]{:S(2)}) %collective-permute-start.2) | collective-permute-done | bytes 139296 | tf_op jit(solution)/shard_map/ppermute | solution.py:21
  25.6 1.8 %copy-done = bf16[2,2048,352]{1,2,0:T(8,128)(2,1)S(1)} copy-done((bf16[2,2048,352]{1,2,0:T(8,128)(2,1)S(1)}, bf16[2,2048,352]{1,2,0:T(8,128)(2,1)}, u32[]{:S(2)}) %copy-start) | copy-done | bytes 2883608
  34.9 3.2 %experts.4 = (f32[128,2048]{1,0:T(8,128)S(1)}, bf16[128,2048]{1,0:T(8,128)(2,1)S(1)}, bf16[256,128]{1,0:T(8,128)(2,1)S(1)}) custom-call(s32[3]{0:T(128)S(1)} %touch.3.place_ref, bf16[32,2176]{1,0:T(8,128)(2,1)S(1)} %pack.1.refs_0_, bf16[32,2176]{1,0:T(8,128)(2,1)S(1)} %collective-permute-done.refs_1_, bf16[32,2176]{1,0:T(8,128)(2,1)S(1)} %collective-permute-done.1.refs_2_, ...), custom_call_target="tpu_custom_call" | custom-call | flops 2214592512 | bytes 8650752 | tf_op jit(solution)/shard_map/experts/pallas_call | solution.py:164
  40.5 3.2 %experts.5 = (f32[128,2048]{1,0:T(8,128)S(1)}, bf16[128,2048]{1,0:T(8,128)(2,1)S(1)}, bf16[256,128]{1,0:T(8,128)(2,1)S(1)}) custom-call(s32[3]{0:T(128)S(1)} %touch.3.place_ref, bf16[64,2176]{1,0:T(8,128)(2,1)S(1)} %constant_dynamic-update-slice_fusion.refs_0_, bf16[64,2176]{1,0:T(8,128)(2,1)S(1)} %collective-permute-done.13.refs_1_, ...), custom_call_target="tpu_custom_call" | custom-call | flops 2214592512 | bytes 8650752 | tf_op jit(solution)/shard_map/experts/pallas_call | solution.py:164
  44.8 3.2 %experts.7 = (f32[128,2048]{1,0:T(8,128)S(1)}, bf16[128,2048]{1,0:T(8,128)(2,1)S(1)}, bf16[256,128]{1,0:T(8,128)(2,1)S(1)}) custom-call(s32[3]{0:T(128)S(1)} %touch.3.place_ref, bf16[32,2176]{1,0:T(8,128)(2,1)S(1)} %collective-permute-done.26.refs_0_, bf16[32,2176]{1,0:T(8,128)(2,1)S(1)} %collective-permute-done.27.refs_1_, ...), custom_call_target="tpu_custom_call" | custom-call | flops 2214592512 | bytes 8650752 | tf_op jit(solution)/shard_map/experts/pallas_call | solution.py:164
  51.0 3.2 %experts.6 = (f32[128,2048]{1,0:T(8,128)S(1)}, bf16[128,2048]{1,0:T(8,128)(2,1)S(1)}, bf16[256,128]{1,0:T(8,128)(2,1)S(1)}) custom-call(s32[3]{0:T(128)S(1)} %touch.3.place_ref, bf16[64,2176]{1,0:T(8,128)(2,1)S(1)} %collective-permute-done.17.refs_0_, bf16[64,2176]{1,0:T(8,128)(2,1)S(1)} %collective-permute-done.18.refs_1_, ...), custom_call_target="tpu_custom_call" | custom-call | flops 2214592512 | bytes 8650752 | tf_op jit(solution)/shard_map/experts/pallas_call | solution.py:164
  61.9 4.5 %collective-permute-done.23 = bf16[64,2048]{1,0:T(8,128)(2,1)S(1)} collective-permute-done((bf16[64,2048]{1,0:T(8,128)(2,1)S(1)}, bf16[64,2048]{1,0:T(8,128)(2,1)S(1)}, u32[]{:S(2)}, u32[]{:S(2)}) %collective-permute-start.23) | collective-permute-done | bytes 262176 | tf_op jit(solution)/shard_map/ppermute | solution.py:21
  69.4 5.4 %collective-permute-done.22 = bf16[64,2048]{1,0:T(8,128)(2,1)S(1)} collective-permute-done((bf16[64,2048]{1,0:T(8,128)(2,1)S(1)}, bf16[64,2048]{1,0:T(8,128)(2,1)S(1)}, u32[]{:S(2)}, u32[]{:S(2)}) %collective-permute-start.22) | collective-permute-done | bytes 262176 | tf_op jit(solution)/shard_map/ppermute | solution.py:21
  74.9 3.4 %collective-permute-start.39 = (bf16[32,2048]{1,0:T(8,128)(2,1)S(1)}, bf16[32,2048]{1,0:T(8,128)(2,1)S(1)}, u32[]{:S(2)}, u32[]{:S(2)}) collective-permute-start(bf16[32,2048]{1,0:T(8,128)(2,1)S(1)} %fusion.8), channel_id=1, source_target_pairs={{0,16},{1,17},{2,18},{3,19},{4,20},{5,21},{6,22},{7,23},{8,24},{9,... | collective-permute-start | bytes 393224 | tf_op jit(solution)/shard_map/ppermute | solution.py:21
  79.0 5.2 %collective-permute-done.39 = bf16[32,2048]{1,0:T(8,128)(2,1)S(1)} collective-permute-done((bf16[32,2048]{1,0:T(8,128)(2,1)S(1)}, bf16[32,2048]{1,0:T(8,128)(2,1)S(1)}, u32[]{:S(2)}, u32[]{:S(2)}) %collective-permute-start.39) | collective-permute-done | bytes 131104 | tf_op jit(solution)/shard_map/ppermute | solution.py:21
  85.7 2.2 %collective-permute-start.48 = (bf16[32,2048]{1,0:T(8,128)(2,1)S(1)}, bf16[32,2048]{1,0:T(8,128)(2,1)S(1)}, u32[]{:S(2)}, u32[]{:S(2)}) collective-permute-start(bf16[32,2048]{1,0:T(8,128)(2,1)S(1)} %fusion.4.refs_0_), channel_id=1, source_target_pairs={{0,8},{1,9},{2,10},{3,11},{4,12},{5,13},{6,14},{7,15},{8,0},{9,1},... | collective-permute-start | bytes 393224 | tf_op jit(solution)/shard_map/ppermute | solution.py:21
  89.6 3.6 %collective-permute-done.47 = bf16[32,2048]{1,0:T(8,128)(2,1)S(1)} collective-permute-done((bf16[32,2048]{1,0:T(8,128)(2,1)S(1)}, bf16[32,2048]{1,0:T(8,128)(2,1)S(1)}, u32[]{:S(2)}, u32[]{:S(2)}) %collective-permute-start.47) | collective-permute-done | bytes 131104 | tf_op jit(solution)/shard_map/ppermute | solution.py:21
  97.3 1.9 %collective-permute-done.42.refs_3_ = bf16[32,2048]{1,0:T(8,128)(2,1)S(1)} collective-permute-done((bf16[32,2048]{1,0:T(8,128)(2,1)S(1)}, bf16[32,2048]{1,0:T(8,128)(2,1)S(1)}, u32[]{:S(2)}, u32[]{:S(2)}) %collective-permute-start.42) | collective-permute-done | bytes 131104 | tf_op jit(solution)/shard_map/ppermute | solution.py:21
  104.0 2.6 %collective-permute-done.56.refs_0_ = bf16[32,2048]{1,0:T(8,128)(2,1)} collective-permute-done((bf16[32,2048]{1,0:T(8,128)(2,1)S(1)}, bf16[32,2048]{1,0:T(8,128)(2,1)}, u32[]{:S(2)}, u32[]{:S(2)}) %collective-permute-start.56) | collective-permute-done | bytes 131104 | tf_op jit(solution)/shard_map/ppermute | solution.py:21
  114.3 2.9 %collective-permute-done.59.refs_3_ = bf16[32,2048]{1,0:T(8,128)(2,1)} collective-permute-done((bf16[32,2048]{1,0:T(8,128)(2,1)}, bf16[32,2048]{1,0:T(8,128)(2,1)}, u32[]{:S(2)}, u32[]{:S(2)}) %collective-permute-start.59) | collective-permute-done | bytes 131104 | tf_op jit(solution)/shard_map/ppermute | solution.py:21
  128.1 2.3 %stats.5 = f32[8,256]{1,0:T(8,128)S(1)} custom-call(s32[1]{0:T(128)} %bitcast.base_ref, bf16[64,2048]{1,0:T(8,128)(2,1)S(1)} %constant_dynamic-update-slice_fusion.2.refs_0_, bf16[64,2048]{1,0:T(8,128)(2,1)} %collective-permute-done.49.refs_1_, bf16[64,2048]{1,0:T(8,128)(2,1)S(1)} %copy-done.8, bf16[64,2048]{1,0:T(8,128)(2,1)} %collective-permute-done.51.refs_3_, ...), custom_call_target="tpu_custom_call" | custom-call | flops 805306368 | bytes 3145728 | tf_op jit(solution)/shard_map/stats/pallas_call | solution.py:213
  131.3 2.5 %stats.7 = f32[8,256]{1,0:T(8,128)S(1)} custom-call(s32[1]{0:T(128)} %bitcast.base_ref, bf16[32,2048]{1,0:T(8,128)(2,1)} %collective-permute-done.56.refs_0_, bf16[32,2048]{1,0:T(8,128)(2,1)} %collective-permute-done.57.refs_1_, bf16[32,2048]{1,0:T(8,128)(2,1)} %collective-permute-done.58.refs_2_, bf16[32,2048]{1,0:T(8,128)(2,1)} %collective-permute-done.59.refs_3_, ...), custom_call_target="tpu_custom_call" | custom-call | flops 805306368 | bytes 3145728 | tf_op jit(solution)/shard_map/stats/pallas_call | solution.py:213
  134.0 2.4 %stats.6 = f32[8,256]{1,0:T(8,128)S(1)} custom-call(s32[1]{0:T(128)} %bitcast.base_ref, bf16[64,2048]{1,0:T(8,128)(2,1)} %collective-permute-done.52.refs_0_, bf16[64,2048]{1,0:T(8,128)(2,1)} %collective-permute-done.53.refs_1_, bf16[64,2048]{1,0:T(8,128)(2,1)} %collective-permute-done.54.refs_2_, bf16[64,2048]{1,0:T(8,128)(2,1)} %collective-permute-done.55.refs_3_, ...), custom_call_target="tpu_custom_call" | custom-call | flops 805306368 | bytes 3145728 | tf_op jit(solution)/shard_map/stats/pallas_call | solution.py:213
  138.3 3.4 %collective-permute-done.65 = f32[3,2,2,2,128]{4,3,0,2,1:T(2,128)S(1)} collective-permute-done((f32[3,2,2,2,128]{4,3,0,2,1:T(2,128)S(1)}, f32[3,2,2,2,128]{4,3,0,2,1:T(2,128)S(1)}, u32[]{:S(2)}, u32[]{:S(2)}) %collective-permute-start.65) | collective-permute-done | bytes 12320 | tf_op jit(solution)/shard_map/ppermute | solution.py:21
  143.5 2.5 %collective-permute-done.66 = f32[3,4,4,32]{3,2,1,0:T(4,128)S(1)} collective-permute-done((f32[3,4,4,32]{3,2,1,0:T(4,128)S(1)}, f32[3,4,4,32]{3,2,1,0:T(4,128)S(1)}, u32[]{:S(2)}, u32[]{:S(2)}) %collective-permute-start.66) | collective-permute-done | bytes 6176 | tf_op jit(solution)/shard_map/ppermute | solution.py:21
  146.4 3.4 %collective-permute-done.67 = f32[3,2,4,32]{3,2,1,0:T(4,128)S(1)} collective-permute-done((f32[3,2,4,32]{3,2,1,0:T(4,128)S(1)}, f32[3,2,4,32]{3,2,1,0:T(4,128)S(1)}, u32[]{:S(2)}, u32[]{:S(2)}) %collective-permute-start.67) | collective-permute-done | bytes 3104 | tf_op jit(solution)/shard_map/ppermute | solution.py:21
  150.4 4.0 %collective-permute-done.68 = f32[3,1,4,32]{3,2,1,0:T(4,128)S(1)} collective-permute-done((f32[3,1,4,32]{3,2,1,0:T(4,128)S(1)}, f32[3,1,4,32]{3,2,1,0:T(4,128)S(1)}, u32[]{:S(2)}, u32[]{:S(2)}) %collective-permute-start.68) | collective-permute-done | bytes 1568 | tf_op jit(solution)/shard_map/ppermute | solution.py:21
  (251 shorter events, 78.6 us)
Async XLA Ops:
  4.1 10.9 %collective-permute-start.11 = (bf16[32,2176]{1,0:T(8,128)(2,1)S(1)}, bf16[32,2176]{1,0:T(8,128)(2,1)S(1)}, u32[]{:S(2)}, u32[]{:S(2)}) collective-permute-start(bf16[32,2176]{1,0:T(8,128)(2,1)S(1)} %pack.1.refs_0_), channel_id=1, source_target_pairs={{0,16},{1,17},{2,18},{3,19},{4,20},{5,21},{6,22},{7,23},{8,24},{9,... | collective-permute-start | bytes 417800 | tf_op jit(solution)/shard_map/ppermute | solution.py:21
  15.7 16.6 %collective-permute-start.13 = (bf16[64,2176]{1,0:T(8,128)(2,1)S(1)}, bf16[64,2176]{1,0:T(8,128)(2,1)S(1)}, u32[]{:S(2)}, u32[]{:S(2)}) collective-permute-start(bf16[64,2176]{1,0:T(8,128)(2,1)S(1)} %constant_dynamic-update-slice_fusion.refs_0_), channel_id=1, source_target_pairs={{0,4},{1,3},{2,6},{3,1},{4,0},{5,7},{6,2},{7,5},{8,12},{9,11},{10,... | collective-permute-start | bytes 835592 | tf_op jit(solution)/shard_map/ppermute | solution.py:21
  17.3 16.1 %collective-permute-start.14 = (bf16[64,2176]{1,0:T(8,128)(2,1)S(1)}, bf16[64,2176]{1,0:T(8,128)(2,1)S(1)}, u32[]{:S(2)}, u32[]{:S(2)}) collective-permute-start(bf16[64,2176]{1,0:T(8,128)(2,1)S(1)} %constant_dynamic-update-slice_fusion.refs_0_), channel_id=1, source_target_pairs={{0,1},{1,0},{2,3},{3,2},{4,5},{5,4},{6,7},{7,6},{8,9},{9,8},{10,11... | collective-permute-start | bytes 835592 | tf_op jit(solution)/shard_map/ppermute | solution.py:21
  22.5 10.8 %collective-permute-start.27 = (bf16[32,2176]{1,0:T(8,128)(2,1)S(1)}, bf16[32,2176]{1,0:T(8,128)(2,1)S(1)}, u32[]{:S(2)}, u32[]{:S(2)}) collective-permute-start(bf16[32,2176]{1,0:T(8,128)(2,1)S(1)} %collective-permute-done.26.refs_0_), channel_id=1, source_target_pairs={{0,4},{1,3},{2,6},{3,1},{4,0},{5,7},{6,2},{7,5},{8,12},{9,11},{10,... | collective-permute-start | bytes 417800 | tf_op jit(solution)/shard_map/ppermute | solution.py:21
  24.1 9.8 %collective-permute-start.6 = (bf16[32,2176]{1,0:T(8,128)(2,1)S(1)}, bf16[32,2176]{1,0:T(8,128)(2,1)S(1)}, u32[]{:S(2)}, u32[]{:S(2)}) collective-permute-start(bf16[32,2176]{1,0:T(8,128)(2,1)S(1)} %collective-permute-done.2.refs_3_), channel_id=1, source_target_pairs={{0,1},{1,0},{2,3},{3,2},{4,5},{5,4},{6,7},{7,6},{8,9},{9,8},{10,11... | collective-permute-start | bytes 417800 | tf_op jit(solution)/shard_map/ppermute | solution.py:21
  24.7 14.0 %collective-permute-start.17 = (bf16[64,2176]{1,0:T(8,128)(2,1)S(1)}, bf16[64,2176]{1,0:T(8,128)(2,1)S(1)}, u32[]{:S(2)}, u32[]{:S(2)}) collective-permute-start(bf16[64,2176]{1,0:T(8,128)(2,1)S(1)} %constant_dynamic-update-slice_fusion.refs_0_), channel_id=1, source_target_pairs={{0,2},{1,5},{2,0},{3,7},{4,6},{5,1},{6,4},{7,3},{8,10},{9,13},{10,... | collective-permute-start | bytes 835592 | tf_op jit(solution)/shard_map/ppermute | solution.py:21
  38.7 10.0 %collective-permute-start.7 = (bf16[128,2048]{1,0:T(8,128)(2,1)S(1)}, bf16[128,2048]{1,0:T(8,128)(2,1)S(1)}, u32[]{:S(2)}, u32[]{:S(2)}) collective-permute-start(bf16[128,2048]{1,0:T(8,128)(2,1)S(1)} %get-tuple-element.18), channel_id=1, source_target_pairs={{0,1},{1,0},{2,3},{3,2},{4,5},{5,4},{6,7},{7,6},{8,9},{9,8},{10,11... | collective-permute-start | bytes 1572872 | tf_op jit(solution)/shard_map/ppermute | solution.py:21
  38.7 9.9 %collective-permute-start.18 = (bf16[64,2176]{1,0:T(8,128)(2,1)S(1)}, bf16[64,2176]{1,0:T(8,128)(2,1)S(1)}, u32[]{:S(2)}, u32[]{:S(2)}) collective-permute-start(bf16[64,2176]{1,0:T(8,128)(2,1)S(1)} %collective-permute-done.13.refs_1_), channel_id=1, source_target_pairs={{0,2},{1,5},{2,0},{3,7},{4,6},{5,1},{6,4},{7,3},{8,10},{9,13},{10,... | collective-permute-start | bytes 835592 | tf_op jit(solution)/shard_map/ppermute | solution.py:21
  44.8 12.2 %collective-permute-start.16 = (bf16[128,2048]{1,0:T(8,128)(2,1)S(1)}, bf16[128,2048]{1,0:T(8,128)(2,1)S(1)}, u32[]{:S(2)}, u32[]{:S(2)}) collective-permute-start(bf16[128,2048]{1,0:T(8,128)(2,1)S(1)} %get-tuple-element.20), channel_id=1, source_target_pairs={{0,1},{1,0},{2,3},{3,2},{4,5},{5,4},{6,7},{7,6},{8,9},{9,8},{10,11... | collective-permute-start | bytes 1572872 | tf_op jit(solution)/shard_map/ppermute | solution.py:21
  49.9 29.1 %collective-permute-start.8 = (bf16[32,2048]{1,0:T(8,128)(2,1)S(1)}, bf16[32,2048]{1,0:T(8,128)(2,1)S(1)}, u32[]{:S(2)}, u32[]{:S(2)}) collective-permute-start(bf16[32,2048]{1,0:T(8,128)(2,1)S(1)} %get-tuple-element.41), channel_id=1, source_target_pairs={{0,2},{1,5},{2,0},{3,7},{4,6},{5,1},{6,4},{7,3},{8,10},{9,13},{10,... | collective-permute-start | bytes 393224 | tf_op jit(solution)/shard_map/ppermute | solution.py:21
  54.4 24.6 %collective-permute-start.10 = (bf16[32,2048]{1,0:T(8,128)(2,1)S(1)}, bf16[32,2048]{1,0:T(8,128)(2,1)S(1)}, u32[]{:S(2)}, u32[]{:S(2)}) collective-permute-start(bf16[32,2048]{1,0:T(8,128)(2,1)S(1)} %fusion.9), channel_id=1, source_target_pairs={{0,4},{1,3},{2,6},{3,1},{4,0},{5,7},{6,2},{7,5},{8,12},{9,11},{10,... | collective-permute-start | bytes 393224 | tf_op jit(solution)/shard_map/ppermute | solution.py:21
  56.9 10.7 %collective-permute-start.35 = (bf16[32,2048]{1,0:T(8,128)(2,1)S(1)}, bf16[32,2048]{1,0:T(8,128)(2,1)S(1)}, u32[]{:S(2)}, u32[]{:S(2)}) collective-permute-start(bf16[32,2048]{1,0:T(8,128)(2,1)S(1)} %get-tuple-element.43), channel_id=1, source_target_pairs={{0,2},{1,5},{2,0},{3,7},{4,6},{5,1},{6,4},{7,3},{8,10},{9,13},{10,... | collective-permute-start | bytes 393224 | tf_op jit(solution)/shard_map/ppermute | solution.py:21
  58.2 8.2 %collective-permute-start.23 = (bf16[64,2048]{1,0:T(8,128)(2,1)S(1)}, bf16[64,2048]{1,0:T(8,128)(2,1)S(1)}, u32[]{:S(2)}, u32[]{:S(2)}) collective-permute-start(bf16[64,2048]{1,0:T(8,128)(2,1)S(1)} %get-tuple-element.46), channel_id=1, source_target_pairs={{0,2},{1,5},{2,0},{3,7},{4,6},{5,1},{6,4},{7,3},{8,10},{9,13},{10,... | collective-permute-start | bytes 786440 | tf_op jit(solution)/shard_map/ppermute | solution.py:21
  66.5 8.3 %collective-permute-start.22 = (bf16[64,2048]{1,0:T(8,128)(2,1)S(1)}, bf16[64,2048]{1,0:T(8,128)(2,1)S(1)}, u32[]{:S(2)}, u32[]{:S(2)}) collective-permute-start(bf16[64,2048]{1,0:T(8,128)(2,1)S(1)} %get-tuple-element.45), channel_id=1, source_target_pairs={{0,2},{1,5},{2,0},{3,7},{4,6},{5,1},{6,4},{7,3},{8,10},{9,13},{10,... | collective-permute-start | bytes 786440 | tf_op jit(solution)/shard_map/ppermute | solution.py:21
  74.9 9.2 %collective-permute-start.39 = (bf16[32,2048]{1,0:T(8,128)(2,1)S(1)}, bf16[32,2048]{1,0:T(8,128)(2,1)S(1)}, u32[]{:S(2)}, u32[]{:S(2)}) collective-permute-start(bf16[32,2048]{1,0:T(8,128)(2,1)S(1)} %fusion.8), channel_id=1, source_target_pairs={{0,16},{1,17},{2,18},{3,19},{4,20},{5,21},{6,22},{7,23},{8,24},{9,... | collective-permute-start | bytes 393224 | tf_op jit(solution)/shard_map/ppermute | solution.py:21
  95.0 12.7 %collective-permute-start.52 = (bf16[64,2048]{1,0:T(8,128)(2,1)S(1)}, bf16[64,2048]{1,0:T(8,128)(2,1)}, u32[]{:S(2)}, u32[]{:S(2)}) collective-permute-start(bf16[64,2048]{1,0:T(8,128)(2,1)S(1)} %constant_dynamic-update-slice_fusion.2.refs_0_), channel_id=1, source_target_pairs={{0,2},{1,5},{2,0},{3,7},{4,6},{5,1},{6,4},{7,3},{8,10},{9,13},{10,... | collective-permute-start | bytes 786440 | tf_op jit(solution)/shard_map/ppermute | solution.py:21
  96.8 10.9 %collective-permute-start.50 = (bf16[64,2048]{1,0:T(8,128)(2,1)S(1)}, bf16[64,2048]{1,0:T(8,128)(2,1)S(1)}, u32[]{:S(2)}, u32[]{:S(2)}) collective-permute-start(bf16[64,2048]{1,0:T(8,128)(2,1)S(1)} %constant_dynamic-update-slice_fusion.2.refs_0_), channel_id=1, source_target_pairs={{0,1},{1,0},{2,3},{3,2},{4,5},{5,4},{6,7},{7,6},{8,9},{9,8},{10,11... | collective-permute-start | bytes 786440 | tf_op jit(solution)/shard_map/ppermute | solution.py:21
  101.5 12.2 %collective-permute-start.53 = (bf16[64,2048]{1,0:T(8,128)(2,1)}, bf16[64,2048]{1,0:T(8,128)(2,1)}, u32[]{:S(2)}, u32[]{:S(2)}) collective-permute-start(bf16[64,2048]{1,0:T(8,128)(2,1)} %collective-permute-done.49.refs_1_), channel_id=1, source_target_pairs={{0,2},{1,5},{2,0},{3,7},{4,6},{5,1},{6,4},{7,3},{8,10},{9,13},{10,... | collective-permute-start | bytes 786440 | tf_op jit(solution)/shard_map/ppermute | solution.py:21
  107.7 9.5 %collective-permute-start.51 = (bf16[64,2048]{1,0:T(8,128)(2,1)}, bf16[64,2048]{1,0:T(8,128)(2,1)}, u32[]{:S(2)}, u32[]{:S(2)}) collective-permute-start(bf16[64,2048]{1,0:T(8,128)(2,1)} %collective-permute-done.49.refs_1_), channel_id=1, source_target_pairs={{0,1},{1,0},{2,3},{3,2},{4,5},{5,4},{6,7},{7,6},{8,9},{9,8},{10,11... | collective-permute-start | bytes 786440 | tf_op jit(solution)/shard_map/ppermute | solution.py:21
  113.7 20.2 %collective-permute-start.54 = (bf16[64,2048]{1,0:T(8,128)(2,1)}, bf16[64,2048]{1,0:T(8,128)(2,1)}, u32[]{:S(2)}, u32[]{:S(2)}) collective-permute-start(bf16[64,2048]{1,0:T(8,128)(2,1)} %collective-permute-done.52.refs_0_), channel_id=1, source_target_pairs={{0,1},{1,0},{2,3},{3,2},{4,5},{5,4},{6,7},{7,6},{8,9},{9,8},{10,11... | collective-permute-start | bytes 786440 | tf_op jit(solution)/shard_map/ppermute | solution.py:21
  113.7 20.2 %collective-permute-start.55 = (bf16[64,2048]{1,0:T(8,128)(2,1)}, bf16[64,2048]{1,0:T(8,128)(2,1)}, u32[]{:S(2)}, u32[]{:S(2)}) collective-permute-start(bf16[64,2048]{1,0:T(8,128)(2,1)} %collective-permute-done.53.refs_1_), channel_id=1, source_target_pairs={{0,1},{1,0},{2,3},{3,2},{4,5},{5,4},{6,7},{7,6},{8,9},{9,8},{10,11... | collective-permute-start | bytes 786440 | tf_op jit(solution)/shard_map/ppermute | solution.py:21
  114.2 16.2 %collective-permute-start.61 = (bf16[32,2048]{1,0:T(8,128)(2,1)}, bf16[32,2048]{1,0:T(8,128)(2,1)}, u32[]{:S(2)}, u32[]{:S(2)}) collective-permute-start(bf16[32,2048]{1,0:T(8,128)(2,1)} %collective-permute-done.57.refs_1_), channel_id=1, source_target_pairs={{0,1},{1,0},{2,3},{3,2},{4,5},{5,4},{6,7},{7,6},{8,9},{9,8},{10,11... | collective-permute-start | bytes 393224 | tf_op jit(solution)/shard_map/ppermute | solution.py:21
  117.2 13.3 %collective-permute-start.62 = (bf16[32,2048]{1,0:T(8,128)(2,1)}, bf16[32,2048]{1,0:T(8,128)(2,1)}, u32[]{:S(2)}, u32[]{:S(2)}) collective-permute-start(bf16[32,2048]{1,0:T(8,128)(2,1)} %collective-permute-done.58.refs_2_), channel_id=1, source_target_pairs={{0,1},{1,0},{2,3},{3,2},{4,5},{5,4},{6,7},{7,6},{8,9},{9,8},{10,11... | collective-permute-start | bytes 393224 | tf_op jit(solution)/shard_map/ppermute | solution.py:21
  117.2 13.3 %collective-permute-start.63 = (bf16[32,2048]{1,0:T(8,128)(2,1)}, bf16[32,2048]{1,0:T(8,128)(2,1)}, u32[]{:S(2)}, u32[]{:S(2)}) collective-permute-start(bf16[32,2048]{1,0:T(8,128)(2,1)} %collective-permute-done.59.refs_3_), channel_id=1, source_target_pairs={{0,1},{1,0},{2,3},{3,2},{4,5},{5,4},{6,7},{7,6},{8,9},{9,8},{10,11... | collective-permute-start | bytes 393224 | tf_op jit(solution)/shard_map/ppermute | solution.py:21
  (80 other events, 376.8 us)
where the time goes:
time: 156 us; the launch traced here: 155 us
  waiting for transfers between devices  52.9 us (34%)
  starting transfers between devices  50.1 us (32%)
  local copies, waits for them, and re-layouts  25.1 us (16%)
  Pallas kernels  24.6 us (16%)
  other arithmetic  1.84 us (1%)
    ppermute x69, waiting for transfers between devices, exchange(): lax.ppermute(value, AXES, [(d, d ^ masks[d & 1]) for d in range(devices)])  52.9 us
    ppermute x69, starting transfers between devices, exchange(): lax.ppermute(value, AXES, [(d, d ^ masks[d & 1]) for d in range(devices)])  50.1 us
    unnamed x72, local copies, waits for them, and re-layouts  23.7 us
    pallas_call x4, Pallas kernels, experts(): pl.pallas_call(functools.partial(expert_kernel, groups=groups), out_shape...  12.9 us
    pallas_call x4, Pallas kernels, row_stats(): pl.pallas_call(functools.partial(stats_kernel, digit=digit), out_shape=ja...  8.53 us
  transfers between devices with their start and end apart: 69, of which 20 were waited for; matrix products, arithmetic and copies ran while one was open for 1% of the time, Pallas kernels for 14%

commit v1 on v0

--- a/solution.py
+++ b/solution.py
@@ -105,26 +105,24 @@
     )(place, tokens, expert_ids, gates, targets)
 
 
-def touch_kernel(place_ref, *refs):
-    for i in range(place_ref.shape[0]):
-        refs[-1][i] = place_ref[i]
-
-
-def touched(place, matrices):
+def touch_kernel(matrix_ref, out_ref):
+    out_ref[...] = jnp.zeros(out_ref.shape, out_ref.dtype)
+
+
+def touched(matrix):
     vmem = pl.BlockSpec(memory_space=pltpu.VMEM)
-    smem = pl.BlockSpec(memory_space=pltpu.SMEM)
     return pl.pallas_call(
         touch_kernel,
-        out_shape=jax.ShapeDtypeStruct(place.shape, place.dtype),
-        in_specs=[smem] + [vmem] * len(matrices),
-        out_specs=smem,
+        out_shape=jax.ShapeDtypeStruct((8, LANES), jnp.float32),
+        in_specs=[vmem],
+        out_specs=vmem,
         compiler_params=pltpu.CompilerParams(vmem_limit_bytes=2**20),
         name="touch",
-    )(place, *matrices)
+    )(matrix)
 
 
 def expert_kernel(place_ref, *refs, groups):
-    pieces = refs[:-8]
+    pieces = refs[:-11]
     gate_ref, up_ref, down_ref, near_out, away_out, info_out, x_ref, hidden_ref = refs[-8:]
     units, width = down_ref.shape
     hid = units // groups
@@ -157,7 +155,7 @@
     away_out[...] = result[rows:].astype(jnp.bfloat16)
 
 
-def experts(place, pieces, matrices, groups):
+def experts(place, pieces, seen, matrices, groups):
     units, width = matrices[2].shape
     rows, total = len(pieces) // 2 * pieces[0].shape[0], pieces[0].shape[1]
     vmem = pl.BlockSpec(memory_space=pltpu.VMEM)
@@ -168,7 +166,7 @@
             jax.ShapeDtypeStruct((rows, width), jnp.bfloat16),
             jax.ShapeDtypeStruct((2 * rows, total - width), jnp.bfloat16),
         ),
-        in_specs=[pl.BlockSpec(memory_space=pltpu.SMEM)] + [vmem] * (len(pieces) + 3),
+        in_specs=[pl.BlockSpec(memory_space=pltpu.SMEM)] + [vmem] * (len(pieces) + 6),
         out_specs=(vmem, vmem, vmem),
         scratch_shapes=[
             pltpu.VMEM((2 * rows, width), jnp.bfloat16),
@@ -180,10 +178,10 @@
         ),
         compiler_params=pltpu.CompilerParams(vmem_limit_bytes=chip_bytes(20, 2 * rows)),
         name="experts",
-    )(place, *pieces, *matrices)
-
-
-def stats_kernel(base_ref, *refs, digit):
+    )(place, *pieces, *seen, *matrices)
+
+
+def stats_kernel(place_ref, *refs, digit):
     pieces = refs[:-3]
     info_ref, weight_ref, out_ref = refs[-3:]
     rows = out_ref.shape[1]
@@ -195,7 +193,7 @@
         place = place + worth * jnp.sum(
             jnp.where(lane == digit + j, info, 0.0), axis=1, keepdims=True
         )
-    place = place.astype(jnp.int32) - base_ref[0]
+    place = place.astype(jnp.int32) - place_ref[3]
     x = jnp.concatenate([ref[...] for ref in pieces], axis=0)
     logits = jnp.dot(x, weight, preferred_element_type=jnp.float32)
     column = lax.broadcasted_iota(jnp.int32, logits.shape, 1)
@@ -207,7 +205,7 @@
     out_ref[...] = flat.T[:8]
 
 
-def row_stats(base, pieces, info, weight, digit):
+def row_stats(where, pieces, info, weight, digit):
     rows = len(pieces) * pieces[0].shape[0]
     vmem = pl.BlockSpec(memory_space=pltpu.VMEM)
     return pl.pallas_call(
@@ -221,7 +219,7 @@
         ),
         compiler_params=pltpu.CompilerParams(vmem_limit_bytes=chip_bytes(12, rows)),
         name="stats",
-    )(base, *pieces, info, weight)
+    )(where, *pieces, info, weight)
 
 
 def layer(tokens, expert_ids, gates, w_gate, w_up, w_down, norm_gain, lm_weight, targets):
@@ -239,7 +237,8 @@
 
     used = 2 * experts_all + 3
     extra = -(-used // LANES) * LANES
-    place = jnp.stack([vocab_index, expert_index * groups, experts_all]).astype(jnp.int32)
+    base = (expert_index * vocab_devs + vocab_index) * lm_weight.shape[1]
+    place = jnp.stack([vocab_index, expert_index * groups, experts_all, base]).astype(jnp.int32)
     payload = packed(place, tokens, expert_ids.T, gates.T, targets.reshape(1, -1), own, extra)
     tokens_own = payload[:, :width]
 
@@ -278,9 +277,9 @@
         return exchange(value.astype(jnp.bfloat16), masks).astype(jnp.float32)
 
     def chip_part(pieces):
-        return experts(place, pieces, matrices, groups)
-
-    place = touched(touched(place, matrices[:2]), matrices[2:])
+        return experts(place, pieces, seen, matrices, groups)
+
+    seen = [touched(matrix) for matrix in matrices]
     parts = spread(payload, chip_part)
     totals = []
     for calls in (parts[:1], parts[1:3], parts[3:]):
@@ -303,8 +302,6 @@
     normed = (resid_f * lax.rsqrt(squares + 1e-06)[:, None] * norm_gain[None, :]).astype(
         jnp.bfloat16
     )
-    base = (expert_index * vocab_devs + vocab_index) * lm_weight.shape[1]
-    base = base.reshape(1).astype(jnp.int32)
 
     def joined(first, second):
         best = jnp.maximum(first[0], second[0])
@@ -314,9 +311,11 @@
     infos = iter([part[2] for part in parts])
 
     def chip_stats(pieces):
-        return row_stats(base, pieces, next(infos), lm_weight, 2 * experts_all)
-
-    got = [q[:3] for q in spread(normed, chip_stats)]
+        return row_stats(place, pieces, next(infos), lm_weight, 2 * experts_all)
+
+    got = spread(normed, chip_stats)
+    got, vocab_index = lax.optimization_barrier((got, vocab_index))
+    got = [q[:3] for q in got]
     table = jnp.concatenate(
         [
             got[0].reshape(3, 2, 2, 2, -1),

time: 156 us -> 143 us (0.917)
  local copies, waits for them, and re-layouts: 25.1 us -> 9.18 us
  waiting for transfers between devices: 52.9 us -> 61.8 us
  Pallas kernels: 24.6 us -> 21.1 us
  starting transfers between devices: 50.1 us -> 48.5 us
    unnamed x72 -> x22, local copies, waits for them, and re-layouts: 23.7 us -> 7.6 us
    ppermute x69, waiting for transfers between devices: 52.9 us -> 61.8 us  [exchange(): lax.ppermute(value, AXES, [(d, d ^ masks[d & 1]) for d in range(devices)])]
    pallas_call x2 -> x3, Pallas kernels: 2.27 us -> 0.01 us  [touched(): pl.pallas_call(touch_kernel, out_shape=jax.ShapeDtypeStruct((8, LANES), j...]
    ppermute x69, starting transfers between devices: 50.1 us -> 48.5 us  [exchange(): lax.ppermute(value, AXES, [(d, d ^ masks[d & 1]) for d in range(devices)])]
  transfers between devices with their start and end apart: 69 -> 69, of which waited for: 20 -> 20; matrix products, arithmetic and copies ran while one was open for 1% -> 1% of each run, Pallas kernels for 14% -> 13%
where the time goes in v1:
time: 143 us
  waiting for transfers between devices  61.8 us (43%)
  starting transfers between devices  48.5 us (34%)
  Pallas kernels  21.1 us (15%)
  local copies, waits for them, and re-layouts  9.18 us (6%)
  other arithmetic  1.7 us (1%)
    ppermute x69, waiting for transfers between devices, exchange(): lax.ppermute(value, AXES, [(d, d ^ masks[d & 1]) for d in range(devices)])  61.8 us
    ppermute x69, starting transfers between devices, exchange(): lax.ppermute(value, AXES, [(d, d ^ masks[d & 1]) for d in range(devices)])  48.5 us
    pallas_call x4, Pallas kernels, experts(): pl.pallas_call(functools.partial(expert_kernel, groups=groups), out_shape...  12.9 us
    unnamed x22, local copies, waits for them, and re-layouts  7.6 us
    pallas_call x4, Pallas kernels, row_stats(): pl.pallas_call(functools.partial(stats_kernel, digit=digit), out_shape=ja...  7.27 us
  transfers between devices with their start and end apart: 69, of which 20 were waited for; matrix products, arithmetic and copies ran while one was open for 1% of the time, Pallas kernels for 13%

profile of v1, /device:TPU:0, one launch (start us, length us, event | category | flops | bytes accessed | tf_op | source)
XLA Modules:
  0.0 142.7 jit_solution(460026688004593177)
XLA Ops:
  4.1 4.1 %collective-permute-start.11 = (bf16[32,2176]{1,0:T(8,128)(2,1)S(1)}, bf16[32,2176]{1,0:T(8,128)(2,1)S(1)}, u32[]{:S(2)}, u32[]{:S(2)}) collective-permute-start(bf16[32,2176]{1,0:T(8,128)(2,1)S(1)} %pack.1.refs_0_), channel_id=1, source_target_pairs={{0,16},{1,17},{2,18},{3,19},{4,20},{5,21},{6,22},{7,23},{8,24},{9,... | collective-permute-start | bytes 417800 | tf_op jit(solution)/shard_map/ppermute | solution.py:21
  12.8 2.2 %collective-permute-done.11 = bf16[32,2176]{1,0:T(8,128)(2,1)S(1)} collective-permute-done((bf16[32,2176]{1,0:T(8,128)(2,1)S(1)}, bf16[32,2176]{1,0:T(8,128)(2,1)S(1)}, u32[]{:S(2)}, u32[]{:S(2)}) %collective-permute-start.11) | collective-permute-done | bytes 139296 | tf_op jit(solution)/shard_map/ppermute | solution.py:21
  20.1 2.5 %collective-permute-done.2.refs_3_ = bf16[32,2176]{1,0:T(8,128)(2,1)S(1)} collective-permute-done((bf16[32,2176]{1,0:T(8,128)(2,1)S(1)}, bf16[32,2176]{1,0:T(8,128)(2,1)S(1)}, u32[]{:S(2)}, u32[]{:S(2)}) %collective-permute-start.2) | collective-permute-done | bytes 139296 | tf_op jit(solution)/shard_map/ppermute | solution.py:21
  32.7 3.2 %experts.4 = (f32[128,2048]{1,0:T(8,128)S(1)}, bf16[128,2048]{1,0:T(8,128)(2,1)S(1)}, bf16[256,128]{1,0:T(8,128)(2,1)S(1)}) custom-call(s32[4]{0:T(128)S(1)} %pad_add_fusion.place_ref, bf16[32,2176]{1,0:T(8,128)(2,1)S(1)} %pack.1.refs_0_, bf16[32,2176]{1,0:T(8,128)(2,1)S(1)} %collective-permute-done.refs_1_, ...), custom_call_target="tpu_custom_call" | custom-call | flops 2214592512 | bytes 8650752 | tf_op jit(solution)/shard_map/experts/pallas_call | solution.py:162
  37.8 3.2 %experts.5 = (f32[128,2048]{1,0:T(8,128)S(1)}, bf16[128,2048]{1,0:T(8,128)(2,1)S(1)}, bf16[256,128]{1,0:T(8,128)(2,1)S(1)}) custom-call(s32[4]{0:T(128)S(1)} %pad_add_fusion.place_ref, bf16[64,2176]{1,0:T(8,128)(2,1)S(1)} %constant_dynamic-update-slice_fusion.refs_0_, bf16[64,2176]{1,0:T(8,128)(2,1)S(1)} %collective-permute-done.13.refs_1_, ...), custom_call_target="tpu_custom_call" | custom-call | flops 2214592512 | bytes 8650752 | tf_op jit(solution)/shard_map/experts/pallas_call | solution.py:162
  41.6 3.2 %experts.7 = (f32[128,2048]{1,0:T(8,128)S(1)}, bf16[128,2048]{1,0:T(8,128)(2,1)S(1)}, bf16[256,128]{1,0:T(8,128)(2,1)S(1)}) custom-call(s32[4]{0:T(128)S(1)} %pad_add_fusion.place_ref, bf16[32,2176]{1,0:T(8,128)(2,1)S(1)} %collective-permute-done.26.refs_0_, bf16[32,2176]{1,0:T(8,128)(2,1)S(1)} %collective-permute-done.27.refs_1_, ...), custom_call_target="tpu_custom_call" | custom-call | flops 2214592512 | bytes 8650752 | tf_op jit(solution)/shard_map/experts/pallas_call | solution.py:162
  47.7 3.2 %experts.6 = (f32[128,2048]{1,0:T(8,128)S(1)}, bf16[128,2048]{1,0:T(8,128)(2,1)S(1)}, bf16[256,128]{1,0:T(8,128)(2,1)S(1)}) custom-call(s32[4]{0:T(128)S(1)} %pad_add_fusion.place_ref, bf16[64,2176]{1,0:T(8,128)(2,1)S(1)} %collective-permute-done.17.refs_0_, bf16[64,2176]{1,0:T(8,128)(2,1)S(1)} %collective-permute-done.18.refs_1_, ...), custom_call_target="tpu_custom_call" | custom-call | flops 2214592512 | bytes 8650752 | tf_op jit(solution)/shard_map/experts/pallas_call | solution.py:162
  58.7 4.5 %collective-permute-done.23 = bf16[64,2048]{1,0:T(8,128)(2,1)S(1)} collective-permute-done((bf16[64,2048]{1,0:T(8,128)(2,1)S(1)}, bf16[64,2048]{1,0:T(8,128)(2,1)S(1)}, u32[]{:S(2)}, u32[]{:S(2)}) %collective-permute-start.23) | collective-permute-done | bytes 262176 | tf_op jit(solution)/shard_map/ppermute | solution.py:21
  66.1 5.3 %collective-permute-done.22 = bf16[64,2048]{1,0:T(8,128)(2,1)S(1)} collective-permute-done((bf16[64,2048]{1,0:T(8,128)(2,1)S(1)}, bf16[64,2048]{1,0:T(8,128)(2,1)S(1)}, u32[]{:S(2)}, u32[]{:S(2)}) %collective-permute-start.22) | collective-permute-done | bytes 262176 | tf_op jit(solution)/shard_map/ppermute | solution.py:21
  71.6 3.4 %collective-permute-start.39 = (bf16[32,2048]{1,0:T(8,128)(2,1)S(1)}, bf16[32,2048]{1,0:T(8,128)(2,1)S(1)}, u32[]{:S(2)}, u32[]{:S(2)}) collective-permute-start(bf16[32,2048]{1,0:T(8,128)(2,1)S(1)} %fusion.8), channel_id=1, source_target_pairs={{0,16},{1,17},{2,18},{3,19},{4,20},{5,21},{6,22},{7,23},{8,24},{9,... | collective-permute-start | bytes 393224 | tf_op jit(solution)/shard_map/ppermute | solution.py:21
  75.6 5.1 %collective-permute-done.39 = bf16[32,2048]{1,0:T(8,128)(2,1)S(1)} collective-permute-done((bf16[32,2048]{1,0:T(8,128)(2,1)S(1)}, bf16[32,2048]{1,0:T(8,128)(2,1)S(1)}, u32[]{:S(2)}, u32[]{:S(2)}) %collective-permute-start.39) | collective-permute-done | bytes 131104 | tf_op jit(solution)/shard_map/ppermute | solution.py:21
  84.3 2.0 %collective-permute-start.48 = (bf16[32,2048]{1,0:T(8,128)(2,1)S(1)}, bf16[32,2048]{1,0:T(8,128)(2,1)S(1)}, u32[]{:S(2)}, u32[]{:S(2)}) collective-permute-start(bf16[32,2048]{1,0:T(8,128)(2,1)S(1)} %fusion.4.refs_0_), channel_id=1, source_target_pairs={{0,8},{1,9},{2,10},{3,11},{4,12},{5,13},{6,14},{7,15},{8,0},{9,1},... | collective-permute-start | bytes 393224 | tf_op jit(solution)/shard_map/ppermute | solution.py:21
  86.3 3.5 %collective-permute-done.47 = bf16[32,2048]{1,0:T(8,128)(2,1)S(1)} collective-permute-done((bf16[32,2048]{1,0:T(8,128)(2,1)S(1)}, bf16[32,2048]{1,0:T(8,128)(2,1)S(1)}, u32[]{:S(2)}, u32[]{:S(2)}) %collective-permute-start.47) | collective-permute-done | bytes 131104 | tf_op jit(solution)/shard_map/ppermute | solution.py:21
  89.8 2.1 %collective-permute-done.48 = bf16[32,2048]{1,0:T(8,128)(2,1)S(1)} collective-permute-done((bf16[32,2048]{1,0:T(8,128)(2,1)S(1)}, bf16[32,2048]{1,0:T(8,128)(2,1)S(1)}, u32[]{:S(2)}, u32[]{:S(2)}) %collective-permute-start.48) | collective-permute-done | bytes 131104 | tf_op jit(solution)/shard_map/ppermute | solution.py:21
  95.2 3.6 %collective-permute-done.42.refs_3_ = bf16[32,2048]{1,0:T(8,128)(2,1)S(1)} collective-permute-done((bf16[32,2048]{1,0:T(8,128)(2,1)S(1)}, bf16[32,2048]{1,0:T(8,128)(2,1)S(1)}, u32[]{:S(2)}, u32[]{:S(2)}) %collective-permute-start.42) | collective-permute-done | bytes 131104 | tf_op jit(solution)/shard_map/ppermute | solution.py:21
  98.7 1.9 %collective-permute-done.49.refs_1_ = bf16[64,2048]{1,0:T(8,128)(2,1)S(1)} collective-permute-done((bf16[64,2048]{1,0:T(8,128)(2,1)S(1)}, bf16[64,2048]{1,0:T(8,128)(2,1)S(1)}, u32[]{:S(2)}, u32[]{:S(2)}) %collective-permute-start.49) | collective-permute-done | bytes 262176 | tf_op jit(solution)/shard_map/ppermute | solution.py:21
  101.2 3.4 %collective-permute-done.56.refs_0_ = bf16[32,2048]{1,0:T(8,128)(2,1)S(1)} collective-permute-done((bf16[32,2048]{1,0:T(8,128)(2,1)S(1)}, bf16[32,2048]{1,0:T(8,128)(2,1)S(1)}, u32[]{:S(2)}, u32[]{:S(2)}) %collective-permute-start.56) | collective-permute-done | bytes 131104 | tf_op jit(solution)/shard_map/ppermute | solution.py:21
  106.9 4.0 %collective-permute-done.57.refs_1_ = bf16[32,2048]{1,0:T(8,128)(2,1)S(1)} collective-permute-done((bf16[32,2048]{1,0:T(8,128)(2,1)S(1)}, bf16[32,2048]{1,0:T(8,128)(2,1)S(1)}, u32[]{:S(2)}, u32[]{:S(2)}) %collective-permute-start.57) | collective-permute-done | bytes 131104 | tf_op jit(solution)/shard_map/ppermute | solution.py:21
  111.6 4.3 %collective-permute-done.59.refs_3_ = bf16[32,2048]{1,0:T(8,128)(2,1)S(1)} collective-permute-done((bf16[32,2048]{1,0:T(8,128)(2,1)S(1)}, bf16[32,2048]{1,0:T(8,128)(2,1)S(1)}, u32[]{:S(2)}, u32[]{:S(2)}) %collective-permute-start.59) | collective-permute-done | bytes 131104 | tf_op jit(solution)/shard_map/ppermute | solution.py:21
  121.9 1.8 %stats.6 = f32[8,256]{1,0:T(8,128)S(1)} custom-call(s32[4]{0:T(128)S(1)} %pad_add_fusion.place_ref, bf16[64,2048]{1,0:T(8,128)(2,1)S(1)} %collective-permute-done.52.refs_0_, bf16[64,2048]{1,0:T(8,128)(2,1)S(1)} %collective-permute-done.53.refs_1_, bf16[64,2048]{1,0:T(8,128)(2,1)S(1)} %collective-permute-done.54.refs_2_, ...), custom_call_target="tpu_custom_call" | custom-call | flops 805306368 | bytes 3145728 | tf_op jit(solution)/shard_map/stats/pallas_call | solution.py:211
  125.7 3.7 %collective-permute-done.65 = f32[3,2,2,2,128]{4,3,0,2,1:T(2,128)S(1)} collective-permute-done((f32[3,2,2,2,128]{4,3,0,2,1:T(2,128)S(1)}, f32[3,2,2,2,128]{4,3,0,2,1:T(2,128)S(1)}, u32[]{:S(2)}, u32[]{:S(2)}) %collective-permute-start.65) | collective-permute-done | bytes 12320 | tf_op jit(solution)/shard_map/ppermute | solution.py:21
  129.8 3.8 %collective-permute-done.66 = f32[3,4,4,32]{3,2,1,0:T(4,128)S(1)} collective-permute-done((f32[3,4,4,32]{3,2,1,0:T(4,128)S(1)}, f32[3,4,4,32]{3,2,1,0:T(4,128)S(1)}, u32[]{:S(2)}, u32[]{:S(2)}) %collective-permute-start.66) | collective-permute-done | bytes 6176 | tf_op jit(solution)/shard_map/ppermute | solution.py:21
  134.0 3.4 %collective-permute-done.67 = f32[3,2,4,32]{3,2,1,0:T(4,128)S(1)} collective-permute-done((f32[3,2,4,32]{3,2,1,0:T(4,128)S(1)}, f32[3,2,4,32]{3,2,1,0:T(4,128)S(1)}, u32[]{:S(2)}, u32[]{:S(2)}) %collective-permute-start.67) | collective-permute-done | bytes 3104 | tf_op jit(solution)/shard_map/ppermute | solution.py:21
  138.3 3.7 %collective-permute-done.68 = f32[3,1,4,32]{3,2,1,0:T(4,128)S(1)} collective-permute-done((f32[3,1,4,32]{3,2,1,0:T(4,128)S(1)}, f32[3,1,4,32]{3,2,1,0:T(4,128)S(1)}, u32[]{:S(2)}, u32[]{:S(2)}) %collective-permute-start.68) | collective-permute-done | bytes 1568 | tf_op jit(solution)/shard_map/ppermute | solution.py:21
  (202 shorter events, 61.0 us)
Async XLA Ops:
  4.1 10.9 %collective-permute-start.11 = (bf16[32,2176]{1,0:T(8,128)(2,1)S(1)}, bf16[32,2176]{1,0:T(8,128)(2,1)S(1)}, u32[]{:S(2)}, u32[]{:S(2)}) collective-permute-start(bf16[32,2176]{1,0:T(8,128)(2,1)S(1)} %pack.1.refs_0_), channel_id=1, source_target_pairs={{0,16},{1,17},{2,18},{3,19},{4,20},{5,21},{6,22},{7,23},{8,24},{9,... | collective-permute-start | bytes 417800 | tf_op jit(solution)/shard_map/ppermute | solution.py:21
  15.7 14.5 %collective-permute-start.13 = (bf16[64,2176]{1,0:T(8,128)(2,1)S(1)}, bf16[64,2176]{1,0:T(8,128)(2,1)S(1)}, u32[]{:S(2)}, u32[]{:S(2)}) collective-permute-start(bf16[64,2176]{1,0:T(8,128)(2,1)S(1)} %constant_dynamic-update-slice_fusion.refs_0_), channel_id=1, source_target_pairs={{0,4},{1,3},{2,6},{3,1},{4,0},{5,7},{6,2},{7,5},{8,12},{9,11},{10,... | collective-permute-start | bytes 835592 | tf_op jit(solution)/shard_map/ppermute | solution.py:21
  17.3 14.0 %collective-permute-start.14 = (bf16[64,2176]{1,0:T(8,128)(2,1)S(1)}, bf16[64,2176]{1,0:T(8,128)(2,1)S(1)}, u32[]{:S(2)}, u32[]{:S(2)}) collective-permute-start(bf16[64,2176]{1,0:T(8,128)(2,1)S(1)} %constant_dynamic-update-slice_fusion.refs_0_), channel_id=1, source_target_pairs={{0,1},{1,0},{2,3},{3,2},{4,5},{5,4},{6,7},{7,6},{8,9},{9,8},{10,11... | collective-permute-start | bytes 835592 | tf_op jit(solution)/shard_map/ppermute | solution.py:21
  22.5 8.7 %collective-permute-start.27 = (bf16[32,2176]{1,0:T(8,128)(2,1)S(1)}, bf16[32,2176]{1,0:T(8,128)(2,1)S(1)}, u32[]{:S(2)}, u32[]{:S(2)}) collective-permute-start(bf16[32,2176]{1,0:T(8,128)(2,1)S(1)} %collective-permute-done.26.refs_0_), channel_id=1, source_target_pairs={{0,4},{1,3},{2,6},{3,1},{4,0},{5,7},{6,2},{7,5},{8,12},{9,11},{10,... | collective-permute-start | bytes 417800 | tf_op jit(solution)/shard_map/ppermute | solution.py:21
  24.7 11.2 %collective-permute-start.17 = (bf16[64,2176]{1,0:T(8,128)(2,1)S(1)}, bf16[64,2176]{1,0:T(8,128)(2,1)S(1)}, u32[]{:S(2)}, u32[]{:S(2)}) collective-permute-start(bf16[64,2176]{1,0:T(8,128)(2,1)S(1)} %constant_dynamic-update-slice_fusion.refs_0_), channel_id=1, source_target_pairs={{0,2},{1,5},{2,0},{3,7},{4,6},{5,1},{6,4},{7,3},{8,10},{9,13},{10,... | collective-permute-start | bytes 835592 | tf_op jit(solution)/shard_map/ppermute | solution.py:21
  35.9 9.5 %collective-permute-start.7 = (bf16[128,2048]{1,0:T(8,128)(2,1)S(1)}, bf16[128,2048]{1,0:T(8,128)(2,1)S(1)}, u32[]{:S(2)}, u32[]{:S(2)}) collective-permute-start(bf16[128,2048]{1,0:T(8,128)(2,1)S(1)} %get-tuple-element.23), channel_id=1, source_target_pairs={{0,1},{1,0},{2,3},{3,2},{4,5},{5,4},{6,7},{7,6},{8,9},{9,8},{10,11... | collective-permute-start | bytes 1572872 | tf_op jit(solution)/shard_map/ppermute | solution.py:21
  36.0 9.3 %collective-permute-start.18 = (bf16[64,2176]{1,0:T(8,128)(2,1)S(1)}, bf16[64,2176]{1,0:T(8,128)(2,1)S(1)}, u32[]{:S(2)}, u32[]{:S(2)}) collective-permute-start(bf16[64,2176]{1,0:T(8,128)(2,1)S(1)} %collective-permute-done.13.refs_1_), channel_id=1, source_target_pairs={{0,2},{1,5},{2,0},{3,7},{4,6},{5,1},{6,4},{7,3},{8,10},{9,13},{10,... | collective-permute-start | bytes 835592 | tf_op jit(solution)/shard_map/ppermute | solution.py:21
  41.5 12.1 %collective-permute-start.16 = (bf16[128,2048]{1,0:T(8,128)(2,1)S(1)}, bf16[128,2048]{1,0:T(8,128)(2,1)S(1)}, u32[]{:S(2)}, u32[]{:S(2)}) collective-permute-start(bf16[128,2048]{1,0:T(8,128)(2,1)S(1)} %get-tuple-element.25), channel_id=1, source_target_pairs={{0,1},{1,0},{2,3},{3,2},{4,5},{5,4},{6,7},{7,6},{8,9},{9,8},{10,11... | collective-permute-start | bytes 1572872 | tf_op jit(solution)/shard_map/ppermute | solution.py:21
  46.6 29.0 %collective-permute-start.8 = (bf16[32,2048]{1,0:T(8,128)(2,1)S(1)}, bf16[32,2048]{1,0:T(8,128)(2,1)S(1)}, u32[]{:S(2)}, u32[]{:S(2)}) collective-permute-start(bf16[32,2048]{1,0:T(8,128)(2,1)S(1)} %get-tuple-element.51), channel_id=1, source_target_pairs={{0,2},{1,5},{2,0},{3,7},{4,6},{5,1},{6,4},{7,3},{8,10},{9,13},{10,... | collective-permute-start | bytes 393224 | tf_op jit(solution)/shard_map/ppermute | solution.py:21
  51.1 24.5 %collective-permute-start.10 = (bf16[32,2048]{1,0:T(8,128)(2,1)S(1)}, bf16[32,2048]{1,0:T(8,128)(2,1)S(1)}, u32[]{:S(2)}, u32[]{:S(2)}) collective-permute-start(bf16[32,2048]{1,0:T(8,128)(2,1)S(1)} %fusion.9), channel_id=1, source_target_pairs={{0,4},{1,3},{2,6},{3,1},{4,0},{5,7},{6,2},{7,5},{8,12},{9,11},{10,... | collective-permute-start | bytes 393224 | tf_op jit(solution)/shard_map/ppermute | solution.py:21
  53.7 10.7 %collective-permute-start.35 = (bf16[32,2048]{1,0:T(8,128)(2,1)S(1)}, bf16[32,2048]{1,0:T(8,128)(2,1)S(1)}, u32[]{:S(2)}, u32[]{:S(2)}) collective-permute-start(bf16[32,2048]{1,0:T(8,128)(2,1)S(1)} %get-tuple-element.53), channel_id=1, source_target_pairs={{0,2},{1,5},{2,0},{3,7},{4,6},{5,1},{6,4},{7,3},{8,10},{9,13},{10,... | collective-permute-start | bytes 393224 | tf_op jit(solution)/shard_map/ppermute | solution.py:21
  63.2 8.2 %collective-permute-start.22 = (bf16[64,2048]{1,0:T(8,128)(2,1)S(1)}, bf16[64,2048]{1,0:T(8,128)(2,1)S(1)}, u32[]{:S(2)}, u32[]{:S(2)}) collective-permute-start(bf16[64,2048]{1,0:T(8,128)(2,1)S(1)} %get-tuple-element.55), channel_id=1, source_target_pairs={{0,2},{1,5},{2,0},{3,7},{4,6},{5,1},{6,4},{7,3},{8,10},{9,13},{10,... | collective-permute-start | bytes 786440 | tf_op jit(solution)/shard_map/ppermute | solution.py:21
  71.6 9.2 %collective-permute-start.39 = (bf16[32,2048]{1,0:T(8,128)(2,1)S(1)}, bf16[32,2048]{1,0:T(8,128)(2,1)S(1)}, u32[]{:S(2)}, u32[]{:S(2)}) collective-permute-start(bf16[32,2048]{1,0:T(8,128)(2,1)S(1)} %fusion.8), channel_id=1, source_target_pairs={{0,16},{1,17},{2,18},{3,19},{4,20},{5,21},{6,22},{7,23},{8,24},{9,... | collective-permute-start | bytes 393224 | tf_op jit(solution)/shard_map/ppermute | solution.py:21
  82.3 10.3 %collective-permute-start.40 = (bf16[32,2048]{1,0:T(8,128)(2,1)S(1)}, bf16[32,2048]{1,0:T(8,128)(2,1)S(1)}, u32[]{:S(2)}, u32[]{:S(2)}) collective-permute-start(bf16[32,2048]{1,0:T(8,128)(2,1)S(1)} %fusion.4.refs_0_), channel_id=1, source_target_pairs={{0,4},{1,3},{2,6},{3,1},{4,0},{5,7},{6,2},{7,5},{8,12},{9,11},{10,... | collective-permute-start | bytes 393224 | tf_op jit(solution)/shard_map/ppermute | solution.py:21
  83.7 10.2 %collective-permute-start.41 = (bf16[32,2048]{1,0:T(8,128)(2,1)S(1)}, bf16[32,2048]{1,0:T(8,128)(2,1)S(1)}, u32[]{:S(2)}, u32[]{:S(2)}) collective-permute-start(bf16[32,2048]{1,0:T(8,128)(2,1)S(1)} %fusion.4.refs_0_), channel_id=1, source_target_pairs={{0,2},{1,5},{2,0},{3,7},{4,6},{5,1},{6,4},{7,3},{8,10},{9,13},{10,... | collective-permute-start | bytes 393224 | tf_op jit(solution)/shard_map/ppermute | solution.py:21
  84.3 10.1 %collective-permute-start.43 = (bf16[32,2048]{1,0:T(8,128)(2,1)S(1)}, bf16[32,2048]{1,0:T(8,128)(2,1)S(1)}, u32[]{:S(2)}, u32[]{:S(2)}) collective-permute-start(bf16[32,2048]{1,0:T(8,128)(2,1)S(1)} %fusion.4.refs_0_), channel_id=1, source_target_pairs={{0,1},{1,0},{2,3},{3,2},{4,5},{5,4},{6,7},{7,6},{8,9},{9,8},{10,11... | collective-permute-start | bytes 393224 | tf_op jit(solution)/shard_map/ppermute | solution.py:21
  92.0 8.7 %collective-permute-start.49 = (bf16[64,2048]{1,0:T(8,128)(2,1)S(1)}, bf16[64,2048]{1,0:T(8,128)(2,1)S(1)}, u32[]{:S(2)}, u32[]{:S(2)}) collective-permute-start(bf16[64,2048]{1,0:T(8,128)(2,1)S(1)} %constant_dynamic-update-slice_fusion.2.refs_0_), channel_id=1, source_target_pairs={{0,4},{1,3},{2,6},{3,1},{4,0},{5,7},{6,2},{7,5},{8,12},{9,11},{10,... | collective-permute-start | bytes 786440 | tf_op jit(solution)/shard_map/ppermute | solution.py:21
  93.8 11.3 %collective-permute-start.50 = (bf16[64,2048]{1,0:T(8,128)(2,1)S(1)}, bf16[64,2048]{1,0:T(8,128)(2,1)S(1)}, u32[]{:S(2)}, u32[]{:S(2)}) collective-permute-start(bf16[64,2048]{1,0:T(8,128)(2,1)S(1)} %constant_dynamic-update-slice_fusion.2.refs_0_), channel_id=1, source_target_pairs={{0,1},{1,0},{2,3},{3,2},{4,5},{5,4},{6,7},{7,6},{8,9},{9,8},{10,11... | collective-permute-start | bytes 786440 | tf_op jit(solution)/shard_map/ppermute | solution.py:21
  94.3 10.8 %collective-permute-start.52 = (bf16[64,2048]{1,0:T(8,128)(2,1)S(1)}, bf16[64,2048]{1,0:T(8,128)(2,1)S(1)}, u32[]{:S(2)}, u32[]{:S(2)}) collective-permute-start(bf16[64,2048]{1,0:T(8,128)(2,1)S(1)} %constant_dynamic-update-slice_fusion.2.refs_0_), channel_id=1, source_target_pairs={{0,2},{1,5},{2,0},{3,7},{4,6},{5,1},{6,4},{7,3},{8,10},{9,13},{10,... | collective-permute-start | bytes 786440 | tf_op jit(solution)/shard_map/ppermute | solution.py:21
  100.6 10.4 %collective-permute-start.53 = (bf16[64,2048]{1,0:T(8,128)(2,1)S(1)}, bf16[64,2048]{1,0:T(8,128)(2,1)S(1)}, u32[]{:S(2)}, u32[]{:S(2)}) collective-permute-start(bf16[64,2048]{1,0:T(8,128)(2,1)S(1)} %collective-permute-done.49.refs_1_), channel_id=1, source_target_pairs={{0,2},{1,5},{2,0},{3,7},{4,6},{5,1},{6,4},{7,3},{8,10},{9,13},{10,... | collective-permute-start | bytes 786440 | tf_op jit(solution)/shard_map/ppermute | solution.py:21
  105.2 10.8 %collective-permute-start.51 = (bf16[64,2048]{1,0:T(8,128)(2,1)S(1)}, bf16[64,2048]{1,0:T(8,128)(2,1)S(1)}, u32[]{:S(2)}, u32[]{:S(2)}) collective-permute-start(bf16[64,2048]{1,0:T(8,128)(2,1)S(1)} %collective-permute-done.49.refs_1_), channel_id=1, source_target_pairs={{0,1},{1,0},{2,3},{3,2},{4,5},{5,4},{6,7},{7,6},{8,9},{9,8},{10,11... | collective-permute-start | bytes 786440 | tf_op jit(solution)/shard_map/ppermute | solution.py:21
  111.0 11.0 %collective-permute-start.54 = (bf16[64,2048]{1,0:T(8,128)(2,1)S(1)}, bf16[64,2048]{1,0:T(8,128)(2,1)S(1)}, u32[]{:S(2)}, u32[]{:S(2)}) collective-permute-start(bf16[64,2048]{1,0:T(8,128)(2,1)S(1)} %collective-permute-done.52.refs_0_), channel_id=1, source_target_pairs={{0,1},{1,0},{2,3},{3,2},{4,5},{5,4},{6,7},{7,6},{8,9},{9,8},{10,11... | collective-permute-start | bytes 786440 | tf_op jit(solution)/shard_map/ppermute | solution.py:21
  111.1 10.8 %collective-permute-start.55 = (bf16[64,2048]{1,0:T(8,128)(2,1)S(1)}, bf16[64,2048]{1,0:T(8,128)(2,1)S(1)}, u32[]{:S(2)}, u32[]{:S(2)}) collective-permute-start(bf16[64,2048]{1,0:T(8,128)(2,1)S(1)} %collective-permute-done.53.refs_1_), channel_id=1, source_target_pairs={{0,1},{1,0},{2,3},{3,2},{4,5},{5,4},{6,7},{7,6},{8,9},{9,8},{10,11... | collective-permute-start | bytes 786440 | tf_op jit(solution)/shard_map/ppermute | solution.py:21
  111.5 8.6 %collective-permute-start.61 = (bf16[32,2048]{1,0:T(8,128)(2,1)S(1)}, bf16[32,2048]{1,0:T(8,128)(2,1)S(1)}, u32[]{:S(2)}, u32[]{:S(2)}) collective-permute-start(bf16[32,2048]{1,0:T(8,128)(2,1)S(1)} %collective-permute-done.57.refs_1_), channel_id=1, source_target_pairs={{0,1},{1,0},{2,3},{3,2},{4,5},{5,4},{6,7},{7,6},{8,9},{9,8},{10,11... | collective-permute-start | bytes 393224 | tf_op jit(solution)/shard_map/ppermute | solution.py:21
  (55 other events, 336.8 us)
